TPU v7x, 256 devices: a whole 4x4x8 slice. The times are simulated.
256 devices in a mesh: fsdp: 32 (over z, y), model: 8 (over x, core).
Axes of the slice: x: 4, y: 4, z: 8, core: 2. Of those that a mesh axis runs over, the one named last changes fastest.
Arguments:
- x_in: bfloat16 [256, 64, 3072], P('fsdp', 'model')
- gain_attn: float32 [2, 3072], replicated
- gain_mlp: float32 [2, 3072], replicated
- rope_cos: float32 [64, 64], replicated
- rope_sin: float32 [64, 64], replicated
- w_q: bfloat16 [2, 3072, 3072], P(None, 'fsdp', 'model')
- w_k: bfloat16 [2, 3072, 1024], P(None, 'fsdp', 'model')
- w_v: bfloat16 [2, 3072, 1024], P(None, 'fsdp', 'model')
- w_o: bfloat16 [2, 3072, 3072], P(None, 'model', 'fsdp')
- w_gate: bfloat16 [2, 3072, 8192], P(None, 'fsdp', 'model')
- w_up: bfloat16 [2, 3072, 8192], P(None, 'fsdp', 'model')
- w_down: bfloat16 [2, 8192, 3072], P(None, 'model', 'fsdp')
Outputs:
- output: bfloat16 [256, 64, 3072], P('fsdp', 'model')
All inputs are finite; a program needn't handle non-finite values.
Results may differ from a plain program's by a relative error of at most 0.02.
Values are sent between devices in bfloat16 or wider.
A program may use at most 768 MiB of HBM per device.

v0:
```python
import jax
import jax.numpy as jnp
from jax import lax
from jax.sharding import PartitionSpec as P

EPS = 1e-5


def rms_norm(seq_rows, gain_vec):
    rows_f = seq_rows.astype(jnp.float32)
    mean_sq = jnp.mean(rows_f * rows_f, axis=-1, keepdims=True)
    return (rows_f * lax.rsqrt(mean_sq + EPS) * gain_vec).astype(jnp.bfloat16)


def rotate(head_vals, cos_b, sin_b):
    half_dim = head_vals.shape[-1] // 2
    heads_f = head_vals.astype(jnp.float32)
    first_half = heads_f[..., :half_dim]
    second_half = heads_f[..., half_dim:]
    return jnp.concatenate([first_half * cos_b - second_half * sin_b, second_half * cos_b + first_half * sin_b], axis=-1).astype(jnp.bfloat16)


def attend(q_proj, k_proj, v_proj, rope_cos, rope_sin, kv_count):
    batch_rows, seq_len, q_width = q_proj.shape
    head_dim = 2 * rope_cos.shape[1]
    group_size = q_width // (head_dim * kv_count)
    q_rot = rotate(q_proj.reshape(batch_rows, seq_len, kv_count, group_size, head_dim), rope_cos[None, :, None, None, :], rope_sin[None, :, None, None, :])
    k_rot = rotate(k_proj.reshape(batch_rows, seq_len, kv_count, head_dim), rope_cos[None, :, None, :], rope_sin[None, :, None, :])
    v_heads = v_proj.reshape(batch_rows, seq_len, kv_count, head_dim)
    scores = jnp.einsum('bqkgd,bskd->bkgqs', q_rot, k_rot, preferred_element_type=jnp.float32) * head_dim ** -0.5
    positions = jnp.arange(seq_len)
    causal = positions[:, None] >= positions[None, :]
    scores = jnp.where(causal, scores, -jnp.inf)
    attn_probs = jax.nn.softmax(scores, axis=-1).astype(jnp.bfloat16)
    attn_out = jnp.einsum('bkgqs,bskd->bqkgd', attn_probs, v_heads, preferred_element_type=jnp.float32).astype(jnp.bfloat16)
    return attn_out.reshape(batch_rows, seq_len, q_width)


def solution(mesh):
    act_spec = P('fsdp', 'model', None)
    col_spec = P(None, 'fsdp', 'model')
    row_spec = P(None, 'model', 'fsdp')

    def device_step(x_in, gain_attn, gain_mlp, rope_cos, rope_sin, w_q, w_k, w_v, w_o, w_gate, w_up, w_down):
        head_dim = 2 * rope_cos.shape[1]
        kv_local = w_k.shape[-1] // head_dim
        residual = x_in
        for layer_idx in range(w_q.shape[0]):
            wq_full = lax.all_gather(w_q[layer_idx], 'fsdp', axis=0, tiled=True)
            wk_full = lax.all_gather(w_k[layer_idx], 'fsdp', axis=0, tiled=True)
            wv_full = lax.all_gather(w_v[layer_idx], 'fsdp', axis=0, tiled=True)
            wo_full = lax.all_gather(w_o[layer_idx], 'fsdp', axis=1, tiled=True)
            normed = rms_norm(residual, gain_attn[layer_idx])
            normed_all = lax.all_gather(normed, 'model', axis=1, tiled=True)
            q_proj = jnp.einsum('bsd,dn->bsn', normed_all, wq_full, preferred_element_type=jnp.float32).astype(jnp.bfloat16)
            k_proj = jnp.einsum('bsd,dn->bsn', normed_all, wk_full, preferred_element_type=jnp.float32).astype(jnp.bfloat16)
            v_proj = jnp.einsum('bsd,dn->bsn', normed_all, wv_full, preferred_element_type=jnp.float32).astype(jnp.bfloat16)
            attn_out = attend(q_proj, k_proj, v_proj, rope_cos, rope_sin, kv_local)
            attn_part = jnp.einsum('bsn,nd->bsd', attn_out, wo_full, preferred_element_type=jnp.float32)
            attn_sum = lax.psum_scatter(attn_part, 'model', scatter_dimension=1, tiled=True)
            mid_rows = (residual.astype(jnp.float32) + attn_sum).astype(jnp.bfloat16)
            wg_full = lax.all_gather(w_gate[layer_idx], 'fsdp', axis=0, tiled=True)
            wu_full = lax.all_gather(w_up[layer_idx], 'fsdp', axis=0, tiled=True)
            wd_full = lax.all_gather(w_down[layer_idx], 'fsdp', axis=1, tiled=True)
            normed_mlp = rms_norm(mid_rows, gain_mlp[layer_idx])
            mlp_in = lax.all_gather(normed_mlp, 'model', axis=1, tiled=True)
            gate_acc = jnp.einsum('bsd,df->bsf', mlp_in, wg_full, preferred_element_type=jnp.float32)
            up_acc = jnp.einsum('bsd,df->bsf', mlp_in, wu_full, preferred_element_type=jnp.float32)
            hidden = (jax.nn.silu(gate_acc) * up_acc).astype(jnp.bfloat16)
            mlp_part = jnp.einsum('bsf,fd->bsd', hidden, wd_full, preferred_element_type=jnp.float32)
            mlp_sum = lax.psum_scatter(mlp_part, 'model', scatter_dimension=1, tiled=True)
            residual = (mid_rows.astype(jnp.float32) + mlp_sum).astype(jnp.bfloat16)
        return residual

    return jax.shard_map(device_step, mesh=mesh, in_specs=(act_spec, P(), P(), P(), P(), col_spec, col_spec, col_spec, row_spec, col_spec, col_spec, row_spec), out_specs=act_spec, check_vma=False)
```

profile of v0, /device:TPU:1, one launch (start us, length us, event | category | flops | bytes accessed | tf_op | source)
XLA Modules:
  0.0 1207.0 jit_solution(7456457589182392810)
XLA Ops:
  14.7 43.5 %all-gather.1 = bf16[1,3072,128]{2,1,0:T(8,128)(2,1)S(1)} all-gather(bf16[1,96,128]{2,1,0:T(8,128)(2,1)S(1)} %get-tuple-element.34), channel_id=3, replica_groups=mesh['fsdp'=32,'model'=8] {'fsdp'}, dimensions={1}, use_global_device_ids=true | all-gather | bytes 811008 | tf_op jit(solution)/shard_map/all_gather | solution.py:50
  58.1 39.4 %all-gather = bf16[1,3072,128]{2,1,0:T(8,128)(2,1)S(1)} all-gather(bf16[1,96,128]{2,1,0:T(8,128)(2,1)S(1)} %get-tuple-element.36), channel_id=2, replica_groups=mesh['fsdp'=32,'model'=8] {'fsdp'}, dimensions={1}, use_global_device_ids=true | all-gather | bytes 811008 | tf_op jit(solution)/shard_map/all_gather | solution.py:51
  97.5 23.9 %all-gather.29.cloned.1.call-done = bf16[8,64,3072]{2,1,0:T(8,128)(2,1)} async-done(((bf16[8,8,3072]{2,1,0:T(8,128)(2,1)}), bf16[8,64,3072]{2,1,0:T(8,128)(2,1)}) %all-gather.29.cloned.1.call-update) | async-done | bytes 3145744 | tf_op jit(solution)/shard_map/all_gather | solution.py:54
  134.8 62.6 %all-gather.39.cloned.1.call-done = bf16[1,384,3072]{1,2,0:T(8,128)(2,1)} async-done(((bf16[1,384,96]{1,2,0:T(8,128)(2,1)}), bf16[1,384,3072]{1,2,0:T(8,128)(2,1)}) %all-gather.39.cloned.1.call-update) | async-done | bytes 2359312 | tf_op jit(solution)/shard_map/all_gather | solution.py:52
  205.4 44.6 %reduce-scatter.5.cloned.1.call-done = f32[8,8,3072]{2,1,0:T(8,128)} async-done(((f32[8,64,3072]{2,1,0:T(8,128)}), f32[8,8,3072]{2,1,0:T(8,128)}) %reduce-scatter.5.cloned.1.call-update) | async-done | bytes 786448 | tf_op jit(solution)/shard_map/reduce_scatter | solution.py:60
  254.1 85.4 %all-gather.43.cloned.1.call-done = bf16[1,3072,1024]{2,1,0:T(8,128)(2,1)} async-done(((bf16[1,96,1024]{2,1,0:T(8,128)(2,1)}), bf16[1,3072,1024]{2,1,0:T(8,128)(2,1)}) %all-gather.43.cloned.1.call-update) | async-done | bytes 6291472 | tf_op jit(solution)/shard_map/all_gather | solution.py:63
  339.6 30.3 %all-gather.31.cloned.1.call-done = bf16[8,64,3072]{2,1,0:T(8,128)(2,1)} async-done(((bf16[8,8,3072]{2,1,0:T(8,128)(2,1)}), bf16[8,64,3072]{2,1,0:T(8,128)(2,1)}) %all-gather.31.cloned.1.call-update) | async-done | bytes 3145744 | tf_op jit(solution)/shard_map/all_gather | solution.py:66
  369.8 6.4 fusion.8
  376.3 82.9 %all-gather.41.cloned.1.call-done = bf16[1,3072,1024]{2,1,0:T(8,128)(2,1)} async-done(((bf16[1,96,1024]{2,1,0:T(8,128)(2,1)}), bf16[1,3072,1024]{2,1,0:T(8,128)(2,1)}) %all-gather.41.cloned.1.call-update) | async-done | bytes 6291472 | tf_op jit(solution)/shard_map/all_gather | solution.py:62
  459.2 87.7 %all-gather.45.cloned.1.call-done = bf16[1,1024,3072]{1,2,0:T(8,128)(2,1)} async-done(((bf16[1,1024,96]{1,2,0:T(8,128)(2,1)}), bf16[1,1024,3072]{1,2,0:T(8,128)(2,1)}) %all-gather.45.cloned.1.call-update) | async-done | bytes 6291472 | tf_op jit(solution)/shard_map/all_gather | solution.py:64
  546.9 15.1 %fusion.2 = f32[8,64,3072]{2,1,0:T(8,128)} fusion(bf16[1,1024,3072]{1,2,0:T(8,128)(2,1)} %all-gather.45.cloned.1.call-done, f32[8,64,1024]{2,1,0:T(8,128)S(1)} %fusion.8, bf16[8,64,3072]{2,1,0:T(8,128)(2,1)} %all-gather.31.cloned.1.call-done, bf16[1,3072,1024]{2,1,0:T(8,128)(2,1)} %all-gather.41.cloned.1.call-done), kind=kOutput, calls=%fused_computation.2 | convolution fusion | flops 6445596672 | bytes 24117248 | tf_op jit(solution)/shard_map/bsf,fd->bsd/dot_general | solution.py:70
  562.6 42.3 %reduce-scatter.7.cloned.1.call-done = f32[8,8,3072]{2,1,0:T(8,128)} async-done(((f32[8,64,3072]{2,1,0:T(8,128)}), f32[8,8,3072]{2,1,0:T(8,128)}) %reduce-scatter.7.cloned.1.call-update) | async-done | bytes 786448 | tf_op jit(solution)/shard_map/reduce_scatter | solution.py:71
  607.8 39.8 %all-gather.8 = bf16[1,3072,128]{2,1,0:T(8,128)(2,1)S(1)} all-gather(bf16[1,96,128]{2,1,0:T(8,128)(2,1)S(1)} %get-tuple-element.33), channel_id=10, replica_groups=mesh['fsdp'=32,'model'=8] {'fsdp'}, dimensions={1}, use_global_device_ids=true | all-gather | bytes 811008 | tf_op jit(solution)/shard_map/all_gather | solution.py:50
  647.6 40.1 %all-gather.7 = bf16[1,3072,128]{2,1,0:T(8,128)(2,1)} all-gather(bf16[1,96,128]{2,1,0:T(8,128)(2,1)S(1)} %get-tuple-element.35), channel_id=9, replica_groups=mesh['fsdp'=32,'model'=8] {'fsdp'}, dimensions={1}, use_global_device_ids=true | all-gather | bytes 811008 | tf_op jit(solution)/shard_map/all_gather | solution.py:51
  687.8 27.5 %all-gather.33.cloned.1.call-done = bf16[8,64,3072]{2,1,0:T(8,128)(2,1)} async-done(((bf16[8,8,3072]{2,1,0:T(8,128)(2,1)}), bf16[8,64,3072]{2,1,0:T(8,128)(2,1)}) %all-gather.33.cloned.1.call-update) | async-done | bytes 3145744 | tf_op jit(solution)/shard_map/all_gather | solution.py:54
  728.7 62.3 %all-gather.49.cloned.1.call-done = bf16[1,384,3072]{1,2,0:T(8,128)(2,1)} async-done(((bf16[1,384,96]{1,2,0:T(8,128)(2,1)}), bf16[1,384,3072]{1,2,0:T(8,128)(2,1)}) %all-gather.49.cloned.1.call-update) | async-done | bytes 2359312 | tf_op jit(solution)/shard_map/all_gather | solution.py:52
  797.8 45.8 %reduce-scatter.9.cloned.1.call-done = f32[8,8,3072]{2,1,0:T(8,128)} async-done(((f32[8,64,3072]{2,1,0:T(8,128)}), f32[8,8,3072]{2,1,0:T(8,128)}) %reduce-scatter.9.cloned.1.call-update) | async-done | bytes 786448 | tf_op jit(solution)/shard_map/reduce_scatter | solution.py:60
  847.4 85.9 %all-gather.53.cloned.1.call-done = bf16[1,3072,1024]{2,1,0:T(8,128)(2,1)} async-done(((bf16[1,96,1024]{2,1,0:T(8,128)(2,1)}), bf16[1,3072,1024]{2,1,0:T(8,128)(2,1)}) %all-gather.53.cloned.1.call-update) | async-done | bytes 6291472 | tf_op jit(solution)/shard_map/all_gather | solution.py:63
  933.3 30.3 %all-gather.35.cloned.1.call-done = bf16[8,64,3072]{2,1,0:T(8,128)(2,1)} async-done(((bf16[8,8,3072]{2,1,0:T(8,128)(2,1)}), bf16[8,64,3072]{2,1,0:T(8,128)(2,1)}) %all-gather.35.cloned.1.call-update) | async-done | bytes 3145744 | tf_op jit(solution)/shard_map/all_gather | solution.py:66
  963.5 6.4 fusion.4
  970.0 82.8 %all-gather.51.cloned.1.call-done = bf16[1,3072,1024]{2,1,0:T(8,128)(2,1)} async-done(((bf16[1,96,1024]{2,1,0:T(8,128)(2,1)}), bf16[1,3072,1024]{2,1,0:T(8,128)(2,1)}) %all-gather.51.cloned.1.call-update) | async-done | bytes 6291472 | tf_op jit(solution)/shard_map/all_gather | solution.py:62
  1052.7 87.6 %all-gather.55.cloned.1.call-done = bf16[1,1024,3072]{1,2,0:T(8,128)(2,1)} async-done(((bf16[1,1024,96]{1,2,0:T(8,128)(2,1)}), bf16[1,1024,3072]{1,2,0:T(8,128)(2,1)}) %all-gather.55.cloned.1.call-update) | async-done | bytes 6291472 | tf_op jit(solution)/shard_map/all_gather | solution.py:64
  1140.3 15.0 %fusion = f32[8,64,3072]{2,1,0:T(8,128)} fusion(bf16[1,1024,3072]{1,2,0:T(8,128)(2,1)} %all-gather.55.cloned.1.call-done, f32[8,64,1024]{2,1,0:T(8,128)S(1)} %fusion.4, bf16[8,64,3072]{2,1,0:T(8,128)(2,1)} %all-gather.35.cloned.1.call-done, bf16[1,3072,1024]{2,1,0:T(8,128)(2,1)} %all-gather.51.cloned.1.call-done), kind=kOutput, calls=%fused_computation | convolution fusion | flops 6445596672 | bytes 24117248 | tf_op jit(solution)/shard_map/bsf,fd->bsd/dot_general | solution.py:70
  1155.3 42.9 %reduce-scatter.11.cloned.1.call-done = f32[8,8,3072]{2,1,0:T(8,128)} async-done(((f32[8,64,3072]{2,1,0:T(8,128)}), f32[8,8,3072]{2,1,0:T(8,128)}) %reduce-scatter.11.cloned.1.call-update) | async-done | bytes 786448 | tf_op jit(solution)/shard_map/reduce_scatter | solution.py:71
  (103 shorter events, 62.8 us)
Async XLA Ops:
  6.5 51.6 %copy-start.7 = (bf16[2,96,128]{2,1,0:T(8,128)(2,1)S(1)}, bf16[2,96,128]{2,1,0:T(8,128)(2,1)}, u32[]{:S(2)}) copy-start(bf16[2,96,128]{2,1,0:T(8,128)(2,1)} %param.19) | copy-start | bytes 147460
  6.5 91.0 %all-gather.37.cloned.1.call-start = ((), (), s32[]{:S(2)}) async-start(), calls=%async_computation.12 | async-start | bytes 2433024 | tf_op jit(solution)/shard_map/all_gather | solution.py:49
  8.2 113.3 %all-gather.29.cloned.1.call-start = ((), (), s32[]{:S(2)}) async-start(), calls=%async_computation.4 | async-start | bytes 3538944 | tf_op jit(solution)/shard_map/all_gather | solution.py:54
  12.2 185.2 %all-gather.39.cloned.1.call-start = ((), (), s32[]{:S(2)}) async-start(), calls=%async_computation.13 | async-start | bytes 2433024 | tf_op jit(solution)/shard_map/all_gather | solution.py:52
  13.8 236.1 %reduce-scatter.5.cloned.1.call-start = ((), (), s32[]{:S(2)}) async-start(), calls=%async_computation.5 | async-start | bytes 7077888 | tf_op jit(solution)/shard_map/reduce_scatter | solution.py:60
  125.8 3.2 copy-start.2
  125.8 3.2 copy-start.3
  203.5 46.5 %copy-start = (bf16[8,8,3072]{2,1,0:T(8,128)(2,1)S(1)}, bf16[8,8,3072]{2,1,0:T(8,128)(2,1)}, u32[]{:S(2)}) copy-start(bf16[8,8,3072]{2,1,0:T(8,128)(2,1)} %param.12) | copy-start | bytes 1179652
  203.5 48.8 %copy-start.5 = (bf16[2,96,1024]{2,1,0:T(8,128)(2,1)S(1)}, bf16[2,96,1024]{2,1,0:T(8,128)(2,1)}, u32[]{:S(2)}) copy-start(bf16[2,96,1024]{2,1,0:T(8,128)(2,1)} %param.21) | copy-start | bytes 1179652
  203.5 49.6 %copy-start.6 = (bf16[2,1024,96]{1,2,0:T(8,128)(2,1)S(1)}, bf16[2,1024,96]{1,2,0:T(8,128)(2,1)}, u32[]{:S(2)}) copy-start(bf16[2,1024,96]{1,2,0:T(8,128)(2,1)} %param.23) | copy-start | bytes 1179652
  203.5 136.0 %all-gather.43.cloned.1.call-start = ((), (), s32[]{:S(2)}) async-start(), calls=%async_computation.15 | async-start | bytes 6488064 | tf_op jit(solution)/shard_map/all_gather | solution.py:63
  205.3 164.5 %all-gather.31.cloned.1.call-start = ((), (), s32[]{:S(2)}) async-start(), calls=%async_computation.6 | async-start | bytes 3538944 | tf_op jit(solution)/shard_map/all_gather | solution.py:66
  252.2 207.0 %all-gather.41.cloned.1.call-start = ((), (), s32[]{:S(2)}) async-start(), calls=%async_computation.14 | async-start | bytes 6488064 | tf_op jit(solution)/shard_map/all_gather | solution.py:62
  253.1 293.8 %all-gather.45.cloned.1.call-start = ((), (), s32[]{:S(2)}) async-start(), calls=%async_computation.16 | async-start | bytes 6488064 | tf_op jit(solution)/shard_map/all_gather | solution.py:64
  253.9 351.0 %reduce-scatter.7.cloned.1.call-start = ((), (), s32[]{:S(2)}) async-start(), calls=%async_computation.7 | async-start | bytes 7077888 | tf_op jit(solution)/shard_map/reduce_scatter | solution.py:71
  562.0 125.8 %all-gather.47.cloned.1.call-start = ((), (), s32[]{:S(2)}) async-start(), calls=%async_computation.17 | async-start | bytes 2433024 | tf_op jit(solution)/shard_map/all_gather | solution.py:49
  562.6 152.7 %all-gather.33.cloned.1.call-start = ((), (), s32[]{:S(2)}) async-start(), calls=%async_computation.8 | async-start | bytes 3538944 | tf_op jit(solution)/shard_map/all_gather | solution.py:54
  607.2 183.8 %all-gather.49.cloned.1.call-start = ((), (), s32[]{:S(2)}) async-start(), calls=%async_computation.18 | async-start | bytes 2433024 | tf_op jit(solution)/shard_map/all_gather | solution.py:52
  607.7 235.9 %reduce-scatter.9.cloned.1.call-start = ((), (), s32[]{:S(2)}) async-start(), calls=%async_computation.9 | async-start | bytes 7077888 | tf_op jit(solution)/shard_map/reduce_scatter | solution.py:60
  797.2 136.1 %all-gather.53.cloned.1.call-start = ((), (), s32[]{:S(2)}) async-start(), calls=%async_computation.20 | async-start | bytes 6488064 | tf_op jit(solution)/shard_map/all_gather | solution.py:63
  797.8 165.7 %all-gather.35.cloned.1.call-start = ((), (), s32[]{:S(2)}) async-start(), calls=%async_computation.10 | async-start | bytes 3538944 | tf_op jit(solution)/shard_map/all_gather | solution.py:66
  845.9 206.8 %all-gather.51.cloned.1.call-start = ((), (), s32[]{:S(2)}) async-start(), calls=%async_computation.19 | async-start | bytes 6488064 | tf_op jit(solution)/shard_map/all_gather | solution.py:62
  846.5 293.8 %all-gather.55.cloned.1.call-start = ((), (), s32[]{:S(2)}) async-start(), calls=%async_computation.21 | async-start | bytes 6488064 | tf_op jit(solution)/shard_map/all_gather | solution.py:64
  847.1 351.1 %reduce-scatter.11.cloned.1.call-start = ((), (), s32[]{:S(2)}) async-start(), calls=%async_computation.11 | async-start | bytes 7077888 | tf_op jit(solution)/shard_map/reduce_scatter | solution.py:71
  (3 other events, 4.0 us)
Sparse Core Ops, SparseCore 0:
  9.9 77.4 all-gather.36
  89.2 32.1 all-gather.28
  124.0 73.2 all-gather.38
  203.6 46.2 reduce-scatter.4
  252.4 87.1 all-gather.42
  341.2 28.5 all-gather.30
  372.4 86.7 all-gather.40
  461.8 85.1 all-gather.44
  562.1 42.7 reduce-scatter.6
  607.3 73.7 all-gather.46
  683.0 32.2 all-gather.32
  717.7 73.2 all-gather.48
  797.3 46.2 reduce-scatter.8
  846.1 87.1 all-gather.52
  934.9 28.5 all-gather.34
  966.0 86.7 all-gather.50
  1055.2 85.1 all-gather.54
  1155.4 42.7 reduce-scatter.10
where the time goes:
time: 1210 us
  waiting for transfers between devices  927 us (77%)
  blocking collectives  163 us (13%)
  matrix products  77.2 us (6%)
  between operations  13.9 us (1%)
  other arithmetic  12.9 us (1%)
    all_gather x2, waiting for transfers between devices, device_step(): wd_full = lax.all_gather(w_down[layer_idx], 'fsdp', axis=1, tiled=True)  175 us
    all_gather x2, waiting for transfers between devices, device_step(): wu_full = lax.all_gather(w_up[layer_idx], 'fsdp', axis=0, tiled=True)  171 us
    all_gather x2, waiting for transfers between devices, device_step(): wg_full = lax.all_gather(w_gate[layer_idx], 'fsdp', axis=0, tiled=True)  166 us
    all_gather x2, waiting for transfers between devices, device_step(): wo_full = lax.all_gather(w_o[layer_idx], 'fsdp', axis=1, tiled=True)  125 us
    reduce_scatter x2, waiting for transfers between devices, device_step(): lax.psum_scatter(attn_part, 'model', scatter_dimension=1, tiled=True)  90.4 us
    reduce_scatter x2, waiting for transfers between devices, device_step(): lax.psum_scatter(mlp_part, 'model', scatter_dimension=1, tiled=True)  85.2 us
    all_gather x2, blocking collectives, device_step(): wk_full = lax.all_gather(w_k[layer_idx], 'fsdp', axis=0, tiled=True)  83.3 us
    all_gather x2, blocking collectives, device_step(): wv_full = lax.all_gather(w_v[layer_idx], 'fsdp', axis=0, tiled=True)  79.5 us
  transfers between devices with their start and end apart: 18, of which 16 were waited for; matrix products, arithmetic and copies ran while one was open for 5% of the time, Pallas kernels for 0%

commit v1 on v0

v1 whole, which is shorter than its diff:
```python
import heapq

import jax
import jax.numpy as jnp
from jax import lax
from jax.experimental import pallas as pl
from jax.experimental.pallas import tpu as pltpu
from jax.sharding import PartitionSpec as P

EPS = 1e-5
MESH = pl.DeviceIdType.MESH
NZ, NY, NX = 8, 4, 4
D = 3072
HD = 128
ROWS = 96
CHUNK = 768
NCH = D // CHUNK
SCALE = HD ** -0.5
F32, BF16 = jnp.float32, jnp.bfloat16

GROUPS = (
    (0, 0, (2, 2, 2, 2)),
    (0, 1024, (3, 3, 5, 5)),
    (0, 3072, (2, 2, 2, 2)),
    (1, 0, (1, 1, 3, 3)),
    (1, 1024, (4, 4, 4, 4)),
    (1, 3072, (2, 2, 2, 2)),
)
WEIGHT = (0.0, 3.5, 3.5, 4.5, 5.5, 6.5)
OFFSET = {"A": (-7.5, 1.5), "B": (0.5, 12.5)}
DEPTH = 3
SIGN = 1
RATE, LAT = 46.0e3, 2.5


def make_slabs():
    slabs = []
    for g, (layer, first, tiles) in enumerate(GROUPS):
        col = first
        for kind, dirn, n in zip("AABB", (1, -1, 1, -1), tiles):
            slabs.append(dict(g=g, layer=layer, c0=col, n=n * 128, kind=kind, dirn=dirn))
            col += n * 128
    return slabs


def hop(slab, t):
    if slab["kind"] == "A":
        return ("y", t, 1) if t < 3 else ("z", t - 3, 4)
    return ("z", t, 1) if t < 7 else ("y", t - 7, 8)


def make_plan(slabs):
    links = [(ax, d) for ax in "yz" for d in (1, -1)]
    busy = {k: 0.0 for k in links}
    queued = {k: 0 for k in links}
    ready = {k: [] for k in links}
    plan, heap, now = [], [], 0.0

    def rank(item):
        slab, t = slabs[item[0]], item[1]
        late = 0 if t < (3 if slab["kind"] == "A" else 7) else 1
        return (WEIGHT[slab["g"]] + OFFSET[slab["kind"]][late], SIGN * t)

    def issue():
        for k in links:
            while ready[k] and queued[k] < DEPTH:
                i, t = ready[k].pop(min(range(len(ready[k])), key=lambda j: rank(ready[k][j])))
                size = hop(slabs[i], t)[2] * ROWS * slabs[i]["n"] * 2
                busy[k] = max(now, busy[k]) + size / RATE
                queued[k] += 1
                plan.append((now, "s", i, t))
                heapq.heappush(heap, (busy[k] + LAT, i, t))

    for i, slab in enumerate(slabs):
        ready[(hop(slab, 0)[0], slab["dirn"])].append((i, 0))
    issue()
    while heap:
        now, i, t = heapq.heappop(heap)
        plan.append((now, "r", i, t))
        queued[(hop(slabs[i], t)[0], slabs[i]["dirn"])] -= 1
        if t < 9:
            ready[(hop(slabs[i], t + 1)[0], slabs[i]["dirn"])].append((i, t + 1))
        issue()
    return plan


SLABS = make_slabs()
PLAN = make_plan(SLABS)


class Pump:
    def __init__(self, place, where, ssem, rsem):
        self.z, self.y, self.m = place
        self.where, self.ssem, self.rsem = where, ssem, rsem
        self.pos, self.clock = 0, 0.0
        self.last = {SLABS[i]["g"]: n for n, (_, kind, i, _) in enumerate(PLAN) if kind == "r"}
        self.left = set(range(len(SLABS)))

    def desc(self, i, t):
        slab = SLABS[i]
        d = slab["dirn"]
        axis, u, blocks = hop(slab, t)
        z, y = self.z, self.y
        ref, base = self.where(slab)
        cols = pl.ds(slab["c0"] - base, slab["n"])
        if axis == "y":
            yi = lax.rem(y - d * u + 2 * NY, NY)
            to = z * NY + lax.rem(y + d + NY, NY)
            part = ref.at[z, yi, :, cols] if blocks == 1 else ref.at[:, yi, :, cols]
        else:
            zi = lax.rem(z - d * u + 2 * NZ, NZ)
            to = lax.rem(z + d + NZ, NZ) * NY + y
            part = ref.at[zi, y, :, cols] if blocks == 1 else ref.at[zi, :, :, cols]
        return pltpu.make_async_remote_copy(
            src_ref=part, dst_ref=part, send_sem=self.ssem.at[i], recv_sem=self.rsem.at[i, t],
            device_id=(to, self.m), device_id_type=MESH)

    def step(self):
        _, kind, i, t = PLAN[self.pos]
        self.pos += 1
        if kind == "r":
            self.desc(i, t).wait_recv()
        else:
            if t > 0:
                self.desc(i, t - 1).wait_send()
            self.desc(i, t).start()

    def until(self, now):
        while self.pos < len(PLAN) and PLAN[self.pos][0] <= now:
            self.step()

    def spend(self, us):
        self.clock += us
        self.until(self.clock)

    def group(self, g):
        self.clock = max(self.clock, PLAN[self.last[g]][0])
        while self.pos <= self.last[g]:
            self.step()
        self.until(self.clock)

    def sent(self, g):
        mine = sorted(i for i in self.left if SLABS[i]["g"] == g)
        end = max(n for n, (_, _, i, _) in enumerate(PLAN) if i in mine)
        while self.pos <= end:
            self.step()
        for i in mine:
            self.desc(i, 9).wait_send()
        self.left -= set(mine)

    def finish(self):
        for g in range(len(GROUPS)):
            if any(SLABS[i]["g"] == g for i in self.left):
                self.sent(g)


def kernel(x_ref, gain_ref, cos_ref, sin_ref, wq, wk, wv, wo, wg, wu, wd,
           y_ref, wlast, w0, w1, h_all, part, cx, rx1, rx2, zbuf, res, stage,
           lsem, csem, ssem, rsem, ag_s, ag_r, rs_s, rs_r):
    f = lax.axis_index("fsdp")
    m = lax.axis_index("model")
    z, y = f // NY, lax.rem(f, NY)
    x, core = m // 2, lax.rem(m, 2)
    xp, xm, x2 = lax.rem(x + 1, NX), lax.rem(x + 3, NX), lax.rem(x + 2, NX)
    other = 1 - core
    to_p, to_m, to_c = (f, xp * 2 + core), (f, xm * 2 + core), (f, x * 2 + other)

    bar = pltpu.get_barrier_semaphore()
    partners = [to_p, to_m, to_c]
    partners += [(z * NY + lax.rem(y + d, NY), m) for d in (1, NY - 1)]
    partners += [(lax.rem(z + d, NZ) * NY + y, m) for d in (1, NZ - 1)]
    for device in partners:
        pl.semaphore_signal(bar, inc=1, device_id=device, device_id_type=MESH)
    pl.semaphore_wait(bar, len(partners))

    loads = [pltpu.make_async_copy(wd.at[1], stage, lsem.at[0])]
    n = 1
    for layer, ref in ((0, w0), (1, w1)):
        col = 0
        for src, width in ((wq, 384), (wk, 128), (wv, 128), (wo, 384), (wg, 1024), (wu, 1024), (wd, 1024)):
            if col + width <= ref.shape[-1]:
                loads.append(pltpu.make_async_copy(src.at[layer], ref.at[z, y, :, pl.ds(col, width)], lsem.at[n]))
                n += 1
            col += width
    for copy in loads:
        copy.start()
    loads[0].wait()
    out = pltpu.make_async_copy(stage, wlast.at[z, y], lsem.at[n])
    out.start()
    for copy in loads[1:]:
        copy.wait()
    out.wait()

    def where(slab):
        if slab["layer"] == 0:
            return w0, 0
        return (w1, 0) if slab["c0"] < 3072 else (wlast, 3072)

    pump = Pump((z, y, m), where, ssem, rsem)
    pump.until(0.0)

    def remote(src, dst, sems, n, device):
        return pltpu.make_async_remote_copy(
            src_ref=src, dst_ref=dst, send_sem=sems[0].at[n], recv_sem=sems[1].at[n],
            device_id=device, device_id_type=MESH)

    lo, hi = pl.ds(0, 32), pl.ds(32, 32)

    def norm(src_ref, gain_row):
        total = jnp.zeros((64, 1), F32)
        for c in range(NCH):
            v = src_ref[:, c * CHUNK:(c + 1) * CHUNK].astype(F32)
            total += jnp.sum(v * v, axis=-1, keepdims=True)
        inv = lax.rsqrt(total * (1.0 / D) + EPS)
        for c in range(NCH):
            cols = slice(c * CHUNK, (c + 1) * CHUNK)
            v = src_ref[:, cols].astype(F32)
            h_all[x, core, :, cols] = (v * inv * gain_ref[gain_row:gain_row + 1, cols]).astype(BF16)

    def gather_rows():
        sems = (ag_s, ag_r)

        def same(i, j, rows, n, device):
            return remote(h_all.at[i, j, rows], h_all.at[i, j, rows], sems, n, device)

        full = pl.ds(0, 64)
        started = [same(x, core, lo, 0, to_p), same(x, core, hi, 1, to_m), same(x, core, full, 2, to_c),
                   same(x, core, hi, 3, to_p), same(x, core, lo, 4, to_m)]
        for copy in started:
            copy.start()

        def go(copy):
            copy.start()
            started.append(copy)

        pump.spend(7.0)
        same(xm, core, lo, 0, to_p).wait_recv()
        go(same(xm, core, lo, 5, to_p))
        go(same(xm, core, lo, 7, to_c))
        same(xp, core, hi, 1, to_p).wait_recv()
        go(same(xp, core, hi, 6, to_m))
        go(same(xp, core, hi, 8, to_c))
        pump.spend(4.0)
        same(xm, core, hi, 3, to_p).wait_recv()
        go(same(xm, core, hi, 9, to_c))
        same(xp, core, lo, 4, to_p).wait_recv()
        go(same(xp, core, lo, 10, to_c))
        pump.spend(4.0)
        same(x2, core, lo, 5, to_p).wait_recv()
        go(same(x2, core, lo, 11, to_c))
        same(x2, core, hi, 6, to_p).wait_recv()
        go(same(x2, core, hi, 12, to_c))
        pump.spend(2.0)
        for i, rows, n in ((x, full, 2), (xm, lo, 7), (xp, hi, 8), (xm, hi, 9), (xp, lo, 10), (x2, lo, 11), (x2, hi, 12)):
            same(i, other, rows, n, to_p).wait_recv()
        for copy in started:
            copy.wait_send()

    def add_rows(product, src_ref, dst_ref):
        sems = (rs_s, rs_r)
        sent = []

        def go(copy):
            copy.start()
            sent.append(copy)

        def cols_of(c):
            return pl.ds(c * CHUNK, CHUNK)

        def cross(c):
            return remote(part.at[:, other, :, cols_of(c)], cx.at[:, :, cols_of(c)], sems, 7 * c, to_c)

        def first(c, side):
            n, rows, to = ((1, lo, to_p), (2, hi, to_m))[side]
            return remote(part.at[x2, core, rows, cols_of(c)], rx1.at[side, :, cols_of(c)], sems, 7 * c + n, to)

        def second(c, side, late):
            n = 3 + 2 * side + late
            rows = (hi, lo)[side ^ late]
            blk, to = ((xp, to_p), (xm, to_m))[side]
            return remote(part.at[blk, core, rows, cols_of(c)], rx2.at[side, rows, cols_of(c)], sems, 7 * c + n, to)

        def stage_b(c):
            cross(c).wait_recv()
            cols = cols_of(c)
            for i in range(NX):
                part[i, core, :, cols] = part[i, core, :, cols] + cx[i, :, cols]
            for side in (0, 1):
                go(first(c, side))
            for side in (0, 1):
                go(second(c, side, 0))

        def stage_c(c):
            cols = cols_of(c)
            for side in (0, 1):
                first(c, side).wait_recv()
                blk, rows = ((xp, lo), (xm, hi))[side]
                part[blk, core, rows, cols] = part[blk, core, rows, cols] + rx1[side, :, cols]
                go(second(c, side, 1))

        def stage_d(c):
            cols = cols_of(c)
            for side in (0, 1):
                for late in (0, 1):
                    second(c, side, late).wait_recv()
            total = part[x, core, :, cols] + rx2[0, :, cols] + rx2[1, :, cols]
            dst_ref[:, cols] = (src_ref[:, cols].astype(F32) + total).astype(BF16)

        for c in range(NCH):
            product(c)
            go(cross(c))
            if c >= 1:
                stage_b(c - 1)
            if c >= 2:
                stage_c(c - 2)
        pump.spend(2.5)
        stage_b(NCH - 1)
        pump.spend(3.0)
        stage_c(NCH - 2)
        pump.spend(5.0)
        stage_c(NCH - 1)
        for c in range(NCH):
            pump.spend(4.0)
            stage_d(c)
        for copy in sent:
            copy.wait_send()

    rows_q = lax.broadcasted_iota(jnp.int32, (64, 64), 0)
    cols_k = lax.broadcasted_iota(jnp.int32, (64, 64), 1)

    def attend(wref):
        for first, width in ((0, 256), (256, 256), (512, 128)):
            h = h_all[...].reshape(512, D)
            w = wref[:, :, :, first:first + width].reshape(D, width)
            acc = jnp.dot(h, w, preferred_element_type=F32)
            part[:, :, :, first:first + width] = acc.astype(BF16).astype(F32).reshape(4, 2, 64, width)
            pump.spend(1.2)

        def one(s, carry):
            rows = pl.ds(pl.multiple_of(s * 8, 8), 8)
            c2, n2 = cos_ref[...], sin_ref[...]

            def head(j):
                return part[:, :, rows, j * HD:(j + 1) * HD].reshape(64, HD)

            def turn(v):
                return (v * c2 + pltpu.roll(v, HD // 2, 1) * n2).astype(BF16)

            k = turn(head(3))
            v = head(4).astype(BF16)
            for j in range(3):
                q = turn(head(j))
                sc = lax.dot_general(q, k, (((1,), (1,)), ((), ())), preferred_element_type=F32) * SCALE
                sc = jnp.where(rows_q >= cols_k, sc, -jnp.inf)
                e = jnp.exp(sc - jnp.max(sc, axis=-1, keepdims=True))
                p = (e / jnp.sum(e, axis=-1, keepdims=True)).astype(BF16)
                o = jnp.dot(p, v, preferred_element_type=F32).astype(BF16)
                part[:, :, rows, j * HD:(j + 1) * HD] = o.astype(F32).reshape(4, 2, 8, HD)
            return carry

        for half in range(2):
            lax.fori_loop(half * 4, half * 4 + 4, one, 0)
            pump.spend(4.0)
        zbuf[:, 0:384] = part[:, :, :, 0:384].reshape(512, 384).astype(BF16)

    def out_product(wref, first, width, us):
        def product(c):
            def plane(i, carry):
                zi = 2 * c + i
                w = wref[zi, :, :, first:first + width].reshape(4 * ROWS, width)
                acc = lax.dot_general(zbuf[:, 0:width], w, (((1,), (1,)), ((), ())), preferred_element_type=F32)
                cols = pl.ds(pl.multiple_of(zi * 384, 128), 384)
                part[:, :, :, cols] = acc.reshape(4, 2, 64, 384)
                return carry

            lax.fori_loop(0, 2, plane, 0)
            pump.spend(us)
        return product

    def mlp_hidden(wref):
        def tile(i, carry):
            h = h_all[...].reshape(512, D)
            c0 = pl.multiple_of(1024 + i * 256, 256)
            c1 = pl.multiple_of(2048 + i * 256, 256)
            g = jnp.dot(h, wref[:, :, :, pl.ds(c0, 256)].reshape(D, 256), preferred_element_type=F32)
            u = jnp.dot(h, wref[:, :, :, pl.ds(c1, 256)].reshape(D, 256), preferred_element_type=F32)
            zbuf[:, pl.ds(pl.multiple_of(i * 256, 256), 256)] = (jax.nn.silu(g) * u).astype(BF16)
            return carry

        for half in range(2):
            lax.fori_loop(half * 2, half * 2 + 2, tile, 0)
            pump.spend(4.5)

    for layer, wref in ((0, w0), (1, w1)):
        src = x_ref if layer == 0 else res
        norm(src, layer)
        pump.spend(1.0)
        gather_rows()
        pump.group(3 * layer)
        attend(wref)
        add_rows(out_product(wref, 640, 384, 0.7), src, res)
        norm(res, 2 + layer)
        pump.spend(1.0)
        gather_rows()
        pump.group(3 * layer + 1)
        mlp_hidden(wref)
        pump.group(3 * layer + 2)
        down = out_product(w0, 3072, 1024, 1.5)
        if layer == 0:
            add_rows(down, res, res)
        else:
            pump.sent(2)
            copies = [pltpu.make_async_copy(wlast.at[2 * c:2 * c + 2], w0.at[2 * c:2 * c + 2, :, :, 3072:4096], csem.at[c])
                      for c in range(NCH)]
            for copy in copies:
                copy.start()

            def last(c):
                copies[c].wait()
                down(c)

            add_rows(last, res, y_ref)
    pump.finish()


def solution(mesh):
    act_spec = P('fsdp', 'model', None)
    col_spec = P(None, 'fsdp', 'model')
    row_spec = P(None, 'model', 'fsdp')

    def device_step(x_in, gain_attn, gain_mlp, rope_cos, rope_sin, w_q, w_k, w_v, w_o, w_gate, w_up, w_down):
        gains = jnp.concatenate([gain_attn, gain_mlp], axis=0)
        cos2 = jnp.concatenate([rope_cos, rope_cos], axis=-1)
        sin2 = jnp.concatenate([-rope_sin, rope_sin], axis=-1)
        wo_t = jnp.swapaxes(w_o, 1, 2)
        wd_t = jnp.swapaxes(w_down, 1, 2)
        vmem = pl.BlockSpec(memory_space=pltpu.VMEM)
        hbm = pl.BlockSpec(memory_space=pltpu.HBM)
        n_slabs = len(SLABS)
        out, _ = pl.pallas_call(
            kernel,
            name="layers",
            out_shape=(jax.ShapeDtypeStruct((64, D), BF16), jax.ShapeDtypeStruct((NZ, NY, ROWS, 1024), BF16)),
            in_specs=[vmem] * 4 + [hbm] * 7,
            out_specs=(vmem, hbm),
            scratch_shapes=[
                pltpu.VMEM((NZ, NY, ROWS, 4096), BF16),
                pltpu.VMEM((NZ, NY, ROWS, 3072), BF16),
                pltpu.VMEM((4, 2, 64, D), BF16),
                pltpu.VMEM((4, 2, 64, D), F32),
                pltpu.VMEM((4, 64, D), F32),
                pltpu.VMEM((2, 32, D), F32),
                pltpu.VMEM((2, 64, D), F32),
                pltpu.VMEM((512, 1024), BF16),
                pltpu.VMEM((64, D), BF16),
                pltpu.VMEM((ROWS, 1024), BF16),
                pltpu.SemaphoreType.DMA((16,)),
                pltpu.SemaphoreType.DMA((NCH,)),
                pltpu.SemaphoreType.DMA((n_slabs,)),
                pltpu.SemaphoreType.DMA((n_slabs, 10)),
                pltpu.SemaphoreType.DMA((13,)),
                pltpu.SemaphoreType.DMA((13,)),
                pltpu.SemaphoreType.DMA((7 * NCH,)),
                pltpu.SemaphoreType.DMA((7 * NCH,)),
            ],
            compiler_params=pltpu.CompilerParams(
                collective_id=0, has_side_effects=True, vmem_limit_bytes=67043328),
        )(x_in.reshape(64, D), gains, cos2, sin2, w_q, w_k, w_v, wo_t, w_gate, w_up, wd_t)
        return out.reshape(x_in.shape)

    return jax.shard_map(device_step, mesh=mesh, in_specs=(act_spec, P(), P(), P(), P(), col_spec, col_spec, col_spec, row_spec, col_spec, col_spec, row_spec), out_specs=act_spec, check_vma=False)
```

time: 1210 us -> 369 us (0.30)
  waiting for transfers between devices: 927 us -> 0 us
  Pallas kernels: 0 us -> 363 us
  blocking collectives: 163 us -> 0 us
  matrix products: 77.2 us -> 0 us
  between operations: 13.9 us -> 0.01 us
    all_gather x14 -> x0, waiting for transfers between devices: 749 us -> none  [the longest x2 175 us: device_step(): wd_full = lax.all_gather(w_down[layer_idx], 'fsdp', axis=1, tiled=True)]
    pallas_call x0 -> x1, Pallas kernels: none -> 363 us  [device_step(): pl.pallas_call(kernel, name='layers', out_shape=(jax.ShapeDtypeStruct((64...]
    reduce_scatter x4 -> x0, waiting for transfers between devices: 176 us -> none  [the longest x2 90.4 us: device_step(): lax.psum_scatter(attn_part, 'model', scatter_dimension=1, tiled=True)]
    all_gather x4 -> x0, blocking collectives: 163 us -> none  [the longest x2 83.3 us: device_step(): wk_full = lax.all_gather(w_k[layer_idx], 'fsdp', axis=0, tiled=True)]
    dot_general x14 -> x0, matrix products: 77.2 us -> none  [the longest x2 30 us: device_step(): jnp.einsum('bsf,fd->bsd', hidden, wd_full, preferred_element_type=jnp.flo...]
  transfers between devices with their start and end apart: 18 -> 0, of which waited for: 16 -> 0; matrix products, arithmetic and copies ran while one was open for 5% -> 0% of each run, Pallas kernels for 0% -> 0%
where the time goes in v1:
time: 369 us; the launch traced here: 368 us
  Pallas kernels  363 us (98%)
  other arithmetic  3.71 us (1%)
    pallas_call x1, Pallas kernels, device_step(): pl.pallas_call(kernel, name='layers', out_shape=(jax.ShapeDtypeStruct((64...  363 us

profile of v1, /device:TPU:1, one launch (start us, length us, event | category | flops | bytes accessed | tf_op | source)
XLA Modules:
  0.0 368.2 jit_solution(514790859078307471)
XLA Ops:
  0.0 0.8 neg.3
  0.8 1.5 pad_maximum_fusion.1
  2.3 1.4 pad_maximum_fusion.gain_ref
  3.7 362.7 %layers.1 = (bf16[64,3072]{1,0:T(8,128)(2,1)}, bf16[8,4,96,1024]{3,2,1,0:T(8,128)(2,1)}) custom-call(bf16[64,3072]{1,0:T(8,128)(2,1)} %bitcast.5, f32[4,3072]{1,0:T(4,128)} %pad_maximum_fusion.gain_ref, f32[64,128]{1,0:T(8,128)} %get-tuple-element.7.cos_ref, f32[64,128]{1,0:T(8,128)} %get-tuple-element.8.sin_ref, bf16[2,96,384]{2,1,0:T(8,128)(2,1)} %wq.1, ...), custom_call_target="tpu_custom_call" | custom-call | tf_op jit(solution)/shard_map/layers/pallas_call | solution.py:440
  366.4 1.8 copy.14

commit v2 on v1

v2 whole, which is shorter than its diff:
```python
import heapq

import jax
import jax.numpy as jnp
from jax import lax
from jax.experimental import pallas as pl
from jax.experimental.pallas import tpu as pltpu
from jax.sharding import PartitionSpec as P

EPS = 1e-5
MESH = pl.DeviceIdType.MESH
NZ, NY, NX = 8, 4, 4
D = 3072
HD = 128
ROWS = 96
CHUNK = 768
NCH = D // CHUNK
SCALE = HD ** -0.5
F32, BF16 = jnp.float32, jnp.bfloat16

GROUPS = (
    (0, 0, (2, 2, 2, 2)),
    (0, 1024, (2, 2, 6, 6)),
    (0, 3072, (2, 2, 2, 2)),
    (1, 0, (2, 2, 2, 2)),
    (1, 1024, (3, 3, 5, 5)),
    (1, 3072, (2, 2, 2, 2)),
)
WEIGHT = (-28.5, -23, -23, -6, 30, 30)
OFFSET = {"A": (-32, 4.5), "B": (-46, 44.5)}
SIGN = 1
AHEAD, MARGIN = 3.0, 4.0
RATE, LAT = 46.3e3, 2.2
ATTEND_US = 3.0
SEND_US, RECEIVE_US = 0.06, 0.04


def make_slabs(groups):
    slabs = []
    for g, (layer, first, tiles) in enumerate(groups):
        col = first
        for kind, dirn, n in zip("AABB", (1, -1, 1, -1), tiles):
            if n:
                slabs.append(dict(g=g, layer=layer, c0=col, n=n * 128, kind=kind, dirn=dirn))
            col += n * 128
    return slabs


def hop(slab, t):
    if slab["kind"] == "A":
        return ("y", t, 1) if t < 3 else ("z", t - 3, 4)
    return ("z", t, 1) if t < 7 else ("y", t - 7, 8)


class Planner:
    def __init__(self, slabs, weight, offset, sign, ahead, margin):
        self.slabs, self.weight, self.offset, self.sign, self.ahead, self.margin = slabs, weight, offset, sign, ahead, margin
        self.spent = 0.0
        self.links = [(ax, d) for ax in "yz" for d in (1, -1)]
        self.busy = {k: 0.0 for k in self.links}
        self.ready = {k: [] for k in self.links}
        self.heap, self.clock = [], 0.0
        self.due = {}
        self.ends = {}
        for i, slab in enumerate(slabs):
            self.ready[(hop(slab, 0)[0], slab["dirn"])].append((i, 0))
            self.due[slab["g"]] = self.due.get(slab["g"], 0) + 10

    def rank(self, item):
        slab, t = self.slabs[item[0]], item[1]
        late = 0 if t < (3 if slab["kind"] == "A" else 7) else 1
        return (self.weight[slab["g"]] + self.offset[slab["kind"]][late], self.sign * t, item)

    def send(self, i, t):
        pass

    def receive(self, i, t):
        pass

    def turn(self):
        while self.heap and self.heap[0][0] <= self.clock:
            _, i, t = heapq.heappop(self.heap)
            self.receive(i, t)
            self.spent += RECEIVE_US
            g = self.slabs[i]["g"]
            self.due[g] -= 1
            self.ends[g] = self.clock
            if t < 9:
                self.ready[(hop(self.slabs[i], t + 1)[0], self.slabs[i]["dirn"])].append((i, t + 1))
        self.issue(self.ahead)

    def issue(self, ahead):
        for k in self.links:
            while self.ready[k] and self.busy[k] - self.clock < ahead:
                item = min(self.ready[k], key=self.rank)
                self.ready[k].remove(item)
                i, t = item
                size = hop(self.slabs[i], t)[2] * ROWS * self.slabs[i]["n"] * 2
                self.busy[k] = max(self.clock, self.busy[k]) + size / RATE
                self.send(i, t)
                self.spent += SEND_US
                heapq.heappush(self.heap, (self.busy[k] + LAT, i, t))

    def fill(self, us):
        self.spent = 0.0
        self.issue(us + self.margin)
        self.clock += self.spent

    def work(self, us):
        self.clock += us
        self.spent = 0.0
        self.turn()
        self.clock += self.spent

    def idle(self, us):
        end = self.clock + us
        while self.heap and self.heap[0][0] <= end:
            self.clock = max(self.clock, self.heap[0][0])
            self.turn()
        self.clock = end

    def group(self, g):
        while self.due[g]:
            self.clock = max(self.clock, self.heap[0][0])
            self.turn()


SLABS = make_slabs(GROUPS)


class Pump(Planner):
    def __init__(self, place, where, before, spare, ssem, rsem):
        super().__init__(SLABS, WEIGHT, OFFSET, SIGN, AHEAD, MARGIN)
        z, y, self.m = place
        self.z, self.y = z, y
        self.where, self.before, self.spare, self.ssem, self.rsem = where, before, spare, ssem, rsem
        self.left = set(range(len(SLABS)))
        self.zs = [z] + [lax.rem(z + u, NZ) for u in range(1, NZ)]
        self.ys = [y] + [lax.rem(y + u, NY) for u in range(1, NY)]
        self.to = {("y", d): z * NY + self.ys[d % NY] for d in (1, -1)}
        self.to.update({("z", d): self.zs[d % NZ] * NY + y for d in (1, -1)})

    def desc(self, i, t):
        slab = SLABS[i]
        d = slab["dirn"]
        axis, u, blocks = hop(slab, t)
        ref, base = self.where(slab)
        cols = pl.ds(slab["c0"] - base, slab["n"])
        if axis == "y":
            yi = self.ys[-d * u % NY]
            part = ref.at[self.z, yi, :, cols] if blocks == 1 else ref.at[:, yi, :, cols]
        else:
            zi = self.zs[-d * u % NZ]
            part = ref.at[zi, self.y, :, cols] if blocks == 1 else ref.at[zi, :, :, cols]
        return pltpu.make_async_remote_copy(
            src_ref=part, dst_ref=part, send_sem=self.ssem.at[i], recv_sem=self.rsem.at[i, t],
            device_id=(self.to[axis, d], self.m), device_id_type=MESH)

    def send(self, i, t):
        if t == 0:
            self.before(SLABS[i])
        self.desc(i, t).start()

    def receive(self, i, t):
        self.desc(i, t).wait_recv()

    def sent(self, g):
        self.group(g)
        for i in sorted(i for i in self.left if SLABS[i]["g"] == g):
            whole = self.spare.at[pl.ds(0, NZ * NY - 1), :, pl.ds(0, SLABS[i]["n"])]
            pltpu.make_async_copy(whole, whole, self.ssem.at[i]).wait()
            self.left.remove(i)

    def finish(self):
        for g in range(len(GROUPS)):
            self.sent(g)


def kernel(x_ref, gain_a, gain_m, cos_ref, sin_ref, wq, wk, wv, wo, wg, wu, wd,
           y_ref, wlast, w0, w1, h_all, part, cx, rx1, rx2, zbuf, res, stage, cos2, sin2,
           lsem, csem, ssem, rsem, ag_s, ag_r, rs_s, rs_r):
    f = lax.axis_index("fsdp")
    m = lax.axis_index("model")
    z, y = f // NY, lax.rem(f, NY)
    x, core = m // 2, lax.rem(m, 2)
    xp, xm, x2 = lax.rem(x + 1, NX), lax.rem(x + 3, NX), lax.rem(x + 2, NX)
    other = 1 - core
    to_p, to_m, to_c = (f, xp * 2 + core), (f, xm * 2 + core), (f, x * 2 + other)

    loads = []
    for layer, ref in ((0, w0), (1, w1)):
        col = 0
        for src, width in ((wq, 384), (wk, 128), (wv, 128), (wo, 384), (wg, 1024), (wu, 1024), (wd, 1024)):
            to = ref.at[z, y, :, pl.ds(col, width)] if col + width <= ref.shape[-1] else stage
            copy = pltpu.make_async_copy(src.at[layer], to, lsem.at[len(loads)])
            copy.start()
            loads.append((layer, col, width, copy))
            col += width
    waited = set()

    def before(slab):
        for n, (layer, col, width, copy) in enumerate(loads):
            if layer == slab["layer"] and col < slab["c0"] + slab["n"] and slab["c0"] < col + width and n not in waited:
                waited.add(n)
                if n < len(loads) - 1:
                    copy.wait()

    bar = pltpu.get_barrier_semaphore()
    partners = [to_p, to_m, to_c]
    partners += [(z * NY + lax.rem(y + d, NY), m) for d in (1, NY - 1)]
    partners += [(lax.rem(z + d, NZ) * NY + y, m) for d in (1, NZ - 1)]
    for device in partners:
        pl.semaphore_signal(bar, inc=1, device_id=device, device_id_type=MESH)

    def norm(src_ref, gain_ref, layer):
        total = jnp.zeros((64, 1), F32)
        for c in range(NCH):
            v = src_ref[:, c * CHUNK:(c + 1) * CHUNK].astype(F32)
            total += jnp.sum(v * v, axis=-1, keepdims=True)
        inv = lax.rsqrt(total * (1.0 / D) + EPS)
        for c in range(NCH):
            cols = slice(c * CHUNK, (c + 1) * CHUNK)
            v = src_ref[:, cols].astype(F32)
            h_all[x, core, :, cols] = (v * inv * gain_ref[layer:layer + 1, cols]).astype(BF16)

    norm(x_ref, gain_a, 0)
    cos2[...] = jnp.concatenate([cos_ref[...], cos_ref[...]], axis=-1)
    sin2[...] = jnp.concatenate([-sin_ref[...], sin_ref[...]], axis=-1)

    loads[-1][3].wait()
    out = pltpu.make_async_copy(stage, wlast.at[z, y], lsem.at[len(loads)])
    out.start()
    pl.semaphore_wait(bar, len(partners))
    out.wait()

    def where(slab):
        if slab["layer"] == 0:
            return w0, 0
        return (w1, 0) if slab["c0"] < 3072 else (wlast, 3072)

    pump = Pump((z, y, m), where, before, wlast.reshape(NZ * NY, ROWS, 1024), ssem, rsem)

    def remote(src, dst, sems, n, device):
        return pltpu.make_async_remote_copy(
            src_ref=src, dst_ref=dst, send_sem=sems[0].at[n], recv_sem=sems[1].at[n],
            device_id=device, device_id_type=MESH)

    lo, hi = pl.ds(0, 32), pl.ds(32, 32)
    leaving = []

    def settle():
        for copy in leaving:
            copy.wait_send()
        leaving.clear()

    def gather_rows():
        sems = (ag_s, ag_r)

        def same(i, j, rows, n, device):
            return remote(h_all.at[i, j, rows], h_all.at[i, j, rows], sems, n, device)

        full = pl.ds(0, 64)
        started = [same(x, core, lo, 0, to_p), same(x, core, hi, 1, to_m), same(x, core, full, 2, to_c),
                   same(x, core, hi, 3, to_p), same(x, core, lo, 4, to_m)]
        for copy in started:
            copy.start()
        pump.turn()
        settle()

        def go(copy):
            copy.start()
            started.append(copy)

        pump.idle(7.0)
        same(xm, core, lo, 0, to_p).wait_recv()
        go(same(xm, core, lo, 5, to_p))
        go(same(xm, core, lo, 7, to_c))
        same(xp, core, hi, 1, to_p).wait_recv()
        go(same(xp, core, hi, 6, to_m))
        go(same(xp, core, hi, 8, to_c))
        pump.idle(4.0)
        same(xm, core, hi, 3, to_p).wait_recv()
        go(same(xm, core, hi, 9, to_c))
        same(xp, core, lo, 4, to_p).wait_recv()
        go(same(xp, core, lo, 10, to_c))
        pump.idle(4.0)
        same(x2, core, lo, 5, to_p).wait_recv()
        go(same(x2, core, lo, 11, to_c))
        same(x2, core, hi, 6, to_p).wait_recv()
        go(same(x2, core, hi, 12, to_c))
        pump.idle(2.0)
        for i, rows, n in ((x, full, 2), (xm, lo, 7), (xp, hi, 8), (xm, hi, 9), (xp, lo, 10), (x2, lo, 11), (x2, hi, 12)):
            same(i, other, rows, n, to_p).wait_recv()
        leaving.extend(started)

    def add_rows(product, src_ref, dst_ref):
        sems = (rs_s, rs_r)
        sent = []

        def go(copy):
            copy.start()
            sent.append(copy)

        def cols_of(c):
            return pl.ds(c * CHUNK, CHUNK)

        def cross(c):
            return remote(part.at[:, other, :, cols_of(c)], cx.at[:, :, cols_of(c)], sems, 7 * c, to_c)

        def first(c, side):
            n, rows, to = ((1, lo, to_p), (2, hi, to_m))[side]
            return remote(part.at[x2, core, rows, cols_of(c)], rx1.at[side, :, cols_of(c)], sems, 7 * c + n, to)

        def second(c, side, late):
            n = 3 + 2 * side + late
            rows = (hi, lo)[side ^ late]
            blk, to = ((xp, to_p), (xm, to_m))[side]
            return remote(part.at[blk, core, rows, cols_of(c)], rx2.at[side, rows, cols_of(c)], sems, 7 * c + n, to)

        def stage_b(c):
            cross(c).wait_recv()
            cols = cols_of(c)
            for i in range(NX):
                part[i, core, :, cols] = part[i, core, :, cols] + cx[i, :, cols]
            for side in (0, 1):
                go(first(c, side))
            for side in (0, 1):
                go(second(c, side, 0))

        def stage_c(c):
            cols = cols_of(c)
            for side in (0, 1):
                first(c, side).wait_recv()
                blk, rows = ((xp, lo), (xm, hi))[side]
                part[blk, core, rows, cols] = part[blk, core, rows, cols] + rx1[side, :, cols]
                go(second(c, side, 1))

        def stage_d(c):
            cols = cols_of(c)
            for side in (0, 1):
                for late in (0, 1):
                    second(c, side, late).wait_recv()
            total = part[x, core, :, cols] + rx2[0, :, cols] + rx2[1, :, cols]
            dst_ref[:, cols] = (src_ref[:, cols].astype(F32) + total).astype(BF16)

        for c in range(NCH):
            product(c)
            go(cross(c))
            if c >= 1:
                stage_b(c - 1)
            if c >= 2:
                stage_c(c - 2)
        pump.idle(1.0)
        settle()
        pump.idle(1.0)
        stage_b(NCH - 1)
        pump.idle(3.0)
        stage_c(NCH - 2)
        pump.idle(5.0)
        stage_c(NCH - 1)
        for c in range(NCH):
            pump.idle((0.5, 4.0, 6.0, 6.0)[c])
            stage_d(c)
        leaving.extend(sent)

    rows_q = lax.broadcasted_iota(jnp.int32, (64, 64), 0)
    cols_k = lax.broadcasted_iota(jnp.int32, (64, 64), 1)
    one_head = (rows_q >= cols_k).astype(F32)
    seen = jnp.concatenate([one_head] * 3, axis=0) > 0.5

    def attend(wref):
        for first, width in ((0, 256), (256, 256), (512, 128)):
            pump.fill(1.2)
            h = h_all[...].reshape(512, D)
            w = wref[:, :, :, first:first + width].reshape(D, width)
            acc = jnp.dot(h, w, preferred_element_type=F32)
            part[:, :, :, first:first + width] = acc.astype(BF16).astype(F32).reshape(4, 2, 64, width)
            pump.work(1.2)

        def pair(i, carry):
            c2, n2 = cos2[...], sin2[...]
            c3, n3 = jnp.concatenate([c2] * 3, axis=0), jnp.concatenate([n2] * 3, axis=0)

            def turn(v, c, n):
                return (v * c + pltpu.roll(v, HD // 2, 1) * n).astype(BF16)

            both = []
            for j in range(2):
                rows = pl.ds(pl.multiple_of(i * 16 + j * 8, 8), 8)
                heads = [part[:, :, rows, h * HD:(h + 1) * HD].reshape(64, HD) for h in range(5)]
                both.append((rows, jnp.concatenate(heads[:3], axis=0), heads[3], heads[4]))
            outs = []
            for rows, q, k, v in both:
                sc = lax.dot_general(turn(q, c3, n3), turn(k, c2, n2), (((1,), (1,)), ((), ())),
                                     preferred_element_type=F32) * SCALE
                sc = jnp.where(seen, sc, -jnp.inf)
                e = jnp.exp(sc - jnp.max(sc, axis=-1, keepdims=True))
                p = (e / jnp.sum(e, axis=-1, keepdims=True)).astype(BF16)
                outs.append(jnp.dot(p, v.astype(BF16), preferred_element_type=F32).astype(BF16).astype(F32))
            for (rows, _, _, _), o in zip(both, outs):
                for h in range(3):
                    part[:, :, rows, h * HD:(h + 1) * HD] = o[h * 64:(h + 1) * 64].reshape(4, 2, 8, HD)
            return carry

        for half in range(2):
            pump.fill(ATTEND_US)
            lax.fori_loop(half * 2, half * 2 + 2, pair, 0)
            pump.work(ATTEND_US)
        zbuf[:, 0:384] = part[:, :, :, 0:384].reshape(512, 384).astype(BF16)

    def out_product(wref, first, width, us):
        def product(c):
            def plane(i, carry):
                zi = 2 * c + i
                w = wref[zi, :, :, first:first + width].reshape(4 * ROWS, width)
                acc = lax.dot_general(zbuf[:, 0:width], w, (((1,), (1,)), ((), ())), preferred_element_type=F32)
                cols = pl.ds(pl.multiple_of(zi * 384, 128), 384)
                part[:, :, :, cols] = acc.reshape(4, 2, 64, 384)
                return carry

            pump.fill(us)
            lax.fori_loop(0, 2, plane, 0)
            pump.work(us)
        return product

    def mlp_hidden(wref):
        def tile(i, carry):
            h = h_all[...].reshape(512, D)
            c0 = pl.multiple_of(1024 + i * 256, 256)
            c1 = pl.multiple_of(2048 + i * 256, 256)
            g = jnp.dot(h, wref[:, :, :, pl.ds(c0, 256)].reshape(D, 256), preferred_element_type=F32)
            u = jnp.dot(h, wref[:, :, :, pl.ds(c1, 256)].reshape(D, 256), preferred_element_type=F32)
            zbuf[:, pl.ds(pl.multiple_of(i * 256, 256), 256)] = (jax.nn.silu(g) * u).astype(BF16)
            return carry

        for half in range(2):
            pump.fill(3.7)
            lax.fori_loop(half * 2, half * 2 + 2, tile, 0)
            pump.work(3.7)

    for layer, wref in ((0, w0), (1, w1)):
        src = x_ref if layer == 0 else res
        if layer:
            norm(src, gain_a, layer)
            pump.work(1.0)
        gather_rows()
        pump.group(3 * layer)
        attend(wref)
        add_rows(out_product(wref, 640, 384, 0.7), src, res)
        norm(res, gain_m, layer)
        pump.work(1.0)
        gather_rows()
        pump.group(3 * layer + 1)
        mlp_hidden(wref)
        pump.group(3 * layer + 2)
        down = out_product(w0, 3072, 1024, 1.5)
        if layer == 0:
            add_rows(down, res, res)
        else:
            pump.sent(2)
            copies = [pltpu.make_async_copy(wlast.at[2 * c:2 * c + 2], w0.at[2 * c:2 * c + 2, :, :, 3072:4096], csem.at[c])
                      for c in range(NCH)]
            for copy in copies:
                copy.start()

            def last(c):
                copies[c].wait()
                down(c)

            add_rows(last, res, y_ref)
    settle()
    pump.finish()


def solution(mesh):
    act_spec = P('fsdp', 'model', None)
    col_spec = P(None, 'fsdp', 'model')
    row_spec = P(None, 'model', 'fsdp')

    def device_step(x_in, gain_attn, gain_mlp, rope_cos, rope_sin, w_q, w_k, w_v, w_o, w_gate, w_up, w_down):
        wo_t = jnp.swapaxes(w_o, 1, 2)
        wd_t = jnp.swapaxes(w_down, 1, 2)
        vmem = pl.BlockSpec(memory_space=pltpu.VMEM)
        hbm = pl.BlockSpec(memory_space=pltpu.HBM)
        n_slabs = len(SLABS)
        out, _ = pl.pallas_call(
            kernel,
            name="layers",
            out_shape=(jax.ShapeDtypeStruct((64, D), BF16), jax.ShapeDtypeStruct((NZ, NY, ROWS, 1024), BF16)),
            in_specs=[vmem] * 5 + [hbm] * 7,
            out_specs=(vmem, hbm),
            scratch_shapes=[
                pltpu.VMEM((NZ, NY, ROWS, 4096), BF16),
                pltpu.VMEM((NZ, NY, ROWS, 3072), BF16),
                pltpu.VMEM((4, 2, 64, D), BF16),
                pltpu.VMEM((4, 2, 64, D), F32),
                pltpu.VMEM((4, 64, D), F32),
                pltpu.VMEM((2, 32, D), F32),
                pltpu.VMEM((2, 64, D), F32),
                pltpu.VMEM((512, 1024), BF16),
                pltpu.VMEM((64, D), BF16),
                pltpu.VMEM((ROWS, 1024), BF16),
                pltpu.VMEM((64, HD), F32),
                pltpu.VMEM((64, HD), F32),
                pltpu.SemaphoreType.DMA((16,)),
                pltpu.SemaphoreType.DMA((NCH,)),
                pltpu.SemaphoreType.DMA((n_slabs,)),
                pltpu.SemaphoreType.DMA((n_slabs, 10)),
                pltpu.SemaphoreType.DMA((13,)),
                pltpu.SemaphoreType.DMA((13,)),
                pltpu.SemaphoreType.DMA((7 * NCH,)),
                pltpu.SemaphoreType.DMA((7 * NCH,)),
            ],
            compiler_params=pltpu.CompilerParams(
                collective_id=0, has_side_effects=True, vmem_limit_bytes=67043328),
        )(x_in.reshape(64, D), gain_attn, gain_mlp, rope_cos, rope_sin, w_q, w_k, w_v, wo_t, w_gate, w_up, wd_t)
        return out.reshape(x_in.shape)

    return jax.shard_map(device_step, mesh=mesh, in_specs=(act_spec, P(), P(), P(), P(), col_spec, col_spec, col_spec, row_spec, col_spec, col_spec, row_spec), out_specs=act_spec, check_vma=False)
```

time: 369 us -> 357 us (0.967)
  Pallas kernels: 363 us -> 355 us
  other arithmetic: 3.71 us -> 0 us
    pallas_call x1, Pallas kernels: 363 us -> 355 us  [device_step(): pl.pallas_call(kernel, name='layers', out_shape=(jax.ShapeDtypeStruct((64...]
where the time goes in v2:
time: 357 us
  Pallas kernels  355 us (99%)
    pallas_call x1, Pallas kernels, device_step(): pl.pallas_call(kernel, name='layers', out_shape=(jax.ShapeDtypeStruct((64...  355 us

profile of v2, /device:TPU:1, one launch (start us, length us, event | category | flops | bytes accessed | tf_op | source)
XLA Modules:
  0.0 356.8 jit_solution(14427820148809414904)
XLA Ops:
  0.0 355.1 %layers.1 = (bf16[64,3072]{1,0:T(8,128)(2,1)}, bf16[8,4,96,1024]{3,2,1,0:T(8,128)(2,1)}) custom-call(bf16[64,3072]{1,0:T(8,128)(2,1)} %bitcast.5, f32[2,3072]{1,0:T(2,128)} %gain_a.1, f32[2,3072]{1,0:T(2,128)} %gain_m.1, f32[64,64]{1,0:T(8,128)} %cos_ref.1, f32[64,64]{1,0:T(8,128)} %sin_ref.1, bf16[2,96,384]{2,1,0:T(8,128)(2,1)} %wq.1, ...), custom_call_target="tpu_custom_call" | custom-call | tf_op jit(solution)/shard_map/layers/pallas_call | solution.py:486
  355.1 1.8 copy.14

commit v3 on v2

--- a/solution.py
+++ b/solution.py
@@ -23,15 +23,15 @@
     (0, 1024, (2, 2, 6, 6)),
     (0, 3072, (2, 2, 2, 2)),
     (1, 0, (2, 2, 2, 2)),
-    (1, 1024, (3, 3, 5, 5)),
-    (1, 3072, (2, 2, 2, 2)),
+    (1, 1024, (4, 4, 4, 4)),
+    (1, 3072, (1, 1, 3, 3)),
 )
-WEIGHT = (-28.5, -23, -23, -6, 30, 30)
-OFFSET = {"A": (-32, 4.5), "B": (-46, 44.5)}
+WEIGHT = (-19.0, -13.5, -8.5, 13.5, 15.0, 43.0)
+OFFSET = {"A": (-39.5, -6.5), "B": (-48.0, 49.0)}
 SIGN = 1
 AHEAD, MARGIN = 3.0, 4.0
+ATTEND_US = 2.3
 RATE, LAT = 46.3e3, 2.2
-ATTEND_US = 3.0
 SEND_US, RECEIVE_US = 0.06, 0.04
 
 
@@ -293,7 +293,7 @@
             same(i, other, rows, n, to_p).wait_recv()
         leaving.extend(started)
 
-    def add_rows(product, src_ref, dst_ref):
+    def add_rows(product, cross_us, src_ref, dst_ref):
         sems = (rs_s, rs_r)
         sent = []
 
@@ -347,19 +347,20 @@
             product(c)
             go(cross(c))
             if c >= 1:
+                pump.idle(cross_us)
                 stage_b(c - 1)
             if c >= 2:
                 stage_c(c - 2)
         pump.idle(1.0)
         settle()
-        pump.idle(1.0)
+        pump.idle(1.5)
         stage_b(NCH - 1)
-        pump.idle(3.0)
+        pump.idle(4.5)
         stage_c(NCH - 2)
-        pump.idle(5.0)
+        pump.idle(4.5)
         stage_c(NCH - 1)
         for c in range(NCH):
-            pump.idle((0.5, 4.0, 6.0, 6.0)[c])
+            pump.idle((0.3, 1.5, 3.0, 3.0)[c])
             stage_d(c)
         leaving.extend(sent)
 
@@ -370,12 +371,12 @@
 
     def attend(wref):
         for first, width in ((0, 256), (256, 256), (512, 128)):
-            pump.fill(1.2)
+            pump.fill(1.0)
             h = h_all[...].reshape(512, D)
             w = wref[:, :, :, first:first + width].reshape(D, width)
             acc = jnp.dot(h, w, preferred_element_type=F32)
             part[:, :, :, first:first + width] = acc.astype(BF16).astype(F32).reshape(4, 2, 64, width)
-            pump.work(1.2)
+            pump.work(1.0)
 
         def pair(i, carry):
             c2, n2 = cos2[...], sin2[...]
@@ -446,7 +447,7 @@
         gather_rows()
         pump.group(3 * layer)
         attend(wref)
-        add_rows(out_product(wref, 640, 384, 0.7), src, res)
+        add_rows(out_product(wref, 640, 384, 0.7), 1.8, src, res)
         norm(res, gain_m, layer)
         pump.work(1.0)
         gather_rows()
@@ -455,7 +456,7 @@
         pump.group(3 * layer + 2)
         down = out_product(w0, 3072, 1024, 1.5)
         if layer == 0:
-            add_rows(down, res, res)
+            add_rows(down, 1.0, res, res)
         else:
             pump.sent(2)
             copies = [pltpu.make_async_copy(wlast.at[2 * c:2 * c + 2], w0.at[2 * c:2 * c + 2, :, :, 3072:4096], csem.at[c])
@@ -467,7 +468,7 @@
                 copies[c].wait()
                 down(c)
 
-            add_rows(last, res, y_ref)
+            add_rows(last, 1.0, res, y_ref)
     settle()
     pump.finish()
 

time: 357 us -> 341 us (0.955)
  Pallas kernels: 355 us -> 340 us
    pallas_call x1, Pallas kernels: 355 us -> 340 us  [device_step(): pl.pallas_call(kernel, name='layers', out_shape=(jax.ShapeDtypeStruct((64...]
where the time goes in v3:
time: 341 us
  Pallas kernels  340 us (100%)
    pallas_call x1, Pallas kernels, device_step(): pl.pallas_call(kernel, name='layers', out_shape=(jax.ShapeDtypeStruct((64...  340 us

profile of v3, /device:TPU:1, one launch (start us, length us, event | category | flops | bytes accessed | tf_op | source)
XLA Modules:
  0.0 341.3 jit_solution(10699089742927140952)
XLA Ops:
  0.0 339.5 %layers.1 = (bf16[64,3072]{1,0:T(8,128)(2,1)}, bf16[8,4,96,1024]{3,2,1,0:T(8,128)(2,1)}) custom-call(bf16[64,3072]{1,0:T(8,128)(2,1)} %bitcast.5, f32[2,3072]{1,0:T(2,128)} %gain_a.1, f32[2,3072]{1,0:T(2,128)} %gain_m.1, f32[64,64]{1,0:T(8,128)} %cos_ref.1, f32[64,64]{1,0:T(8,128)} %sin_ref.1, bf16[2,96,384]{2,1,0:T(8,128)(2,1)} %wq.1, ...), custom_call_target="tpu_custom_call" | custom-call | tf_op jit(solution)/shard_map/layers/pallas_call | solution.py:487
  339.5 1.8 copy.14

commit v4 on v3

--- a/solution.py
+++ b/solution.py
@@ -20,16 +20,16 @@
 
 GROUPS = (
     (0, 0, (2, 2, 2, 2)),
-    (0, 1024, (2, 2, 6, 6)),
+    (0, 1024, (3, 1, 6, 6)),
     (0, 3072, (2, 2, 2, 2)),
-    (1, 0, (2, 2, 2, 2)),
-    (1, 1024, (4, 4, 4, 4)),
-    (1, 3072, (1, 1, 3, 3)),
+    (1, 0, (1, 2, 3, 2)),
+    (1, 1024, (5, 5, 3, 3)),
+    (1, 3072, (1, 2, 2, 3)),
 )
-WEIGHT = (-19.0, -13.5, -8.5, 13.5, 15.0, 43.0)
-OFFSET = {"A": (-39.5, -6.5), "B": (-48.0, 49.0)}
+WEIGHT = (-99.0, -94.5, -56.5, -43.0, 35.0, 35.0)
+OFFSET = {"A": (-50.0, 47.0), "B": (-16.0, 14.5)}
 SIGN = 1
-AHEAD, MARGIN = 3.0, 4.0
+AHEAD, MARGIN = 2.5, 1.5
 ATTEND_US = 2.3
 RATE, LAT = 46.3e3, 2.2
 SEND_US, RECEIVE_US = 0.06, 0.04
@@ -293,7 +293,7 @@
             same(i, other, rows, n, to_p).wait_recv()
         leaving.extend(started)
 
-    def add_rows(product, cross_us, src_ref, dst_ref):
+    def add_rows(product, cross_us, src_ref, dst_ref, last=False):
         sems = (rs_s, rs_r)
         sent = []
 
@@ -361,6 +361,11 @@
         stage_c(NCH - 1)
         for c in range(NCH):
             pump.idle((0.3, 1.5, 3.0, 3.0)[c])
+            if last and c == NCH - 1:
+                pump.finish()
+                for copy in sent:
+                    copy.wait_send()
+                sent.clear()
             stage_d(c)
         leaving.extend(sent)
 
@@ -464,13 +469,11 @@
             for copy in copies:
                 copy.start()
 
-            def last(c):
+            def final(c):
                 copies[c].wait()
                 down(c)
 
-            add_rows(last, 1.0, res, y_ref)
-    settle()
-    pump.finish()
+            add_rows(final, 1.0, res, y_ref, last=True)
 
 
 def solution(mesh):

time: 341 us -> 340 us (level)
  no operation moved by 1% of the time
where the time goes in v4:
time: 340 us
  Pallas kernels  338 us (99%)
    pallas_call x1, Pallas kernels, device_step(): pl.pallas_call(kernel, name='layers', out_shape=(jax.ShapeDtypeStruct((64...  338 us

profile of v4, /device:TPU:1, one launch (start us, length us, event | category | flops | bytes accessed | tf_op | source)
XLA Modules:
  0.0 340.0 jit_solution(8229681698381845700)
XLA Ops:
  0.0 338.2 %layers.1 = (bf16[64,3072]{1,0:T(8,128)(2,1)}, bf16[8,4,96,1024]{3,2,1,0:T(8,128)(2,1)}) custom-call(bf16[64,3072]{1,0:T(8,128)(2,1)} %bitcast.5, f32[2,3072]{1,0:T(2,128)} %gain_a.1, f32[2,3072]{1,0:T(2,128)} %gain_m.1, f32[64,64]{1,0:T(8,128)} %cos_ref.1, f32[64,64]{1,0:T(8,128)} %sin_ref.1, bf16[2,96,384]{2,1,0:T(8,128)(2,1)} %wq.1, ...), custom_call_target="tpu_custom_call" | custom-call | tf_op jit(solution)/shard_map/layers/pallas_call | solution.py:490
  338.2 1.8 copy.14
